TPU v7x, 32 devices: a whole 2x2x4 slice. The times are simulated.
32 devices in a mesh: row: 8 (over z, core), col: 4 (over y, x).
Axes of the slice: x: 2, y: 2, z: 4, core: 2. Of those that a mesh axis runs over, the one named last changes fastest.
Arguments:
- signal: float32 [128, 128, 256], P(None, 'row', 'col'), may hold values from -6 to 6
- symbol_x: float32 [128], replicated, may hold values from 0.3 to 3
- symbol_y: float32 [128], replicated, may hold values from 0.3 to 3
- symbol_z: float32 [256], replicated, may hold values from 0.3 to 3
Outputs:
- modes: float32 [128, 128, 256], P('row', 'col')
All inputs are finite; a program needn't handle non-finite values.
Results may differ from a plain program's by a relative error of at most 0.0003.
Values sent between devices are 32-bit elements.
A program may use at most 64 MiB of HBM per device.

v0:
```python
import jax
import jax.numpy as jnp
from jax import lax
from jax.sharding import PartitionSpec as P


def mode_table(count):
    rank = jnp.arange(count)
    angle = 2.0 * jnp.pi / count * (rank[:, None] * rank[None, :] % count).astype(jnp.float32)
    return (jnp.cos(angle) + jnp.sin(angle)) * count ** (-0.5)


def transform_dim(values, dim):
    moved = jnp.tensordot(
        values, mode_table(values.shape[dim]), axes=([dim], [0]), precision=lax.Precision.HIGHEST
    )
    return jnp.moveaxis(moved, -1, dim)


def on_device(signal, symbol_x, symbol_y, symbol_z):

    def first_leg(part_values):
        part_values = transform_dim(part_values, 0)
        part_values = lax.all_to_all(part_values, "row", split_axis=0, concat_axis=1, tiled=True)
        part_values = transform_dim(part_values, 1)
        return part_values

    block_values = first_leg(signal)
    block_values = lax.all_to_all(block_values, "col", split_axis=1, concat_axis=2, tiled=True)
    block_values = transform_dim(block_values, 2)
    share_x = block_values.shape[0]
    part_x = lax.dynamic_slice_in_dim(symbol_x, lax.axis_index("row") * share_x, share_x)
    share_y = block_values.shape[1]
    part_y = lax.dynamic_slice_in_dim(symbol_y, lax.axis_index("col") * share_y, share_y)
    symbol = part_x[:, None, None] + part_y[None, :, None] + symbol_z[None, None, :]
    block_values = block_values * ((1.0 - 0.2 * symbol) / (1.0 + 0.2 * symbol))
    return block_values


def solution(mesh):
    placed = (P(None, "row", "col"), P(), P(), P())
    return jax.shard_map(
        on_device, mesh=mesh, in_specs=placed, out_specs=P("row", "col", None), check_vma=False
    )
```

profile of v0, /device:TPU:0, one launch (start us, length us, event | category | flops | bytes accessed | tf_op | source)
XLA Modules:
  0.0 49.0 jit_solution(2675580543085098439)
XLA Ops:
  0.0 0.0 copy-start
  0.0 1.0 %copy-done = f32[128,16,64]{0,2,1:T(8,128)S(1)} copy-done((f32[128,16,64]{0,2,1:T(8,128)S(1)}, f32[128,16,64]{0,2,1:T(8,128)}, u32[]{:S(2)}) %copy-start) | copy-done | bytes 524312
  1.0 0.8 %fusion.26 = f32[128,1024]{0,1:S(1)} fusion(f32[128,1024]{0,1:T(8,128)S(1)} %bitcast.22), kind=kOutput, calls=%fused_computation.32 | convolution fusion | flops 201588736 | bytes 1048576
  1.9 0.5 %copy.12 = f32[128,16,64]{2,1,0:T(8,128)S(1)} copy(f32[128,16,64]{0,2,1:T(8,128)S(1)} %bitcast.27) | data formatting | bytes 1048576 | tf_op jit(solution)/shard_map/dot_general | solution.py:14
  2.4 0.7 %reshape.37 = f32[8,1,16384]{2,1,0:T(1,128)S(1)} reshape(f32[128,16,64]{2,1,0:T(8,128)S(1)} %copy.12) | data formatting | bytes 1048576
  3.1 21.6 %all_to_all.36 = f32[8,1,16384]{2,1,0:T(1,128)S(1)} all-to-all(f32[8,1,16384]{2,1,0:T(1,128)S(1)} %reshape.37), channel_id=1, replica_groups=mesh['row'=8,'col'=4] {'row'}, dimensions={0} | all-to-all | bytes 1048576 | tf_op jit(solution)/shard_map/all_to_all | solution.py:24
  24.7 0.5 %broadcast.76 = f32[]{:T(128)} broadcast(f32[]{:T(128)} %constant.105), dimensions={} | broadcast | bytes 8 | tf_op jit(solution)/shard_map/all_to_all | solution.py:24
  25.2 1.8 %reduce = f32[8,16384]{1,0:T(8,128)S(1)} reduce(f32[8,1,16384]{2,1,0:T(1,128)S(1)} %all_to_all.36, f32[]{:T(128)} %broadcast.76), dimensions={1}, to_apply=%all_to_all.26.reduce_sub_computation | reduce | bytes 1048580 | tf_op jit(solution)/shard_map/all_to_all | solution.py:24
  27.0 0.4 reshape.38
  27.4 0.1 copy.13
  27.5 1.9 %convolution_bitcast_fusion = f32[16,128,64]{1,2,0:T(8,128)S(1)} fusion(f32[16,128,64]{2,1,0:T(8,128)S(1)} %bitcast.25), kind=kOutput, calls=%fused_computation | convolution fusion | flops 201588736 | bytes 1048576 | tf_op jit(solution)/shard_map/dot_general | solution.py:14
  29.4 0.5 %copy.15 = f32[16,128,64]{2,0,1:T(8,128)S(1)} copy(f32[16,128,64]{1,2,0:T(8,128)S(1)} %convolution_bitcast_fusion) | data formatting | bytes 1048576 | tf_op jit(solution)/shard_map/transpose | solution.py:17
  29.9 1.4 %reshape.39 = f32[4,1,32768]{2,1,0:T(1,128)} reshape(f32[128,16,64]{2,1,0:T(8,128)S(1)} %bitcast.23) | data formatting | bytes 1048576
  31.4 3.7 %all-to-all-start.1 = ((f32[4,1,32768]{2,1,0:T(1,128)}), f32[4,1,32768]{2,1,0:T(1,128)S(1)}, u32[]{:S(2)}, u32[]{:S(2)}) async-start(f32[4,1,32768]{2,1,0:T(1,128)} %reshape.39), calls=%async_computation.1 | async-start | bytes 1048576 | tf_op jit(solution)/shard_map/all_to_all | solution.py:29
  35.1 0.0 copy-start.2
  35.1 0.7 %copy-done.2 = f32[128]{0:T(128)S(1)} copy-done((f32[128]{0:T(128)S(1)}, f32[128]{0:T(128)}, u32[]{:S(2)}) %copy-start.2) | copy-done | bytes 536
  35.7 0.1 dynamic_slice.7
  35.8 0.0 copy-start.3
  35.8 0.7 %copy-done.3 = f32[128]{0:T(128)S(1)} copy-done((f32[128]{0:T(128)S(1)}, f32[128]{0:T(128)}, u32[]{:S(2)}) %copy-start.3) | copy-done | bytes 536
  36.5 0.1 dynamic_slice.6
  36.5 0.1 broadcast_add_fusion
  36.6 6.0 %all-to-all-done.1 = f32[4,1,32768]{2,1,0:T(1,128)S(1)} async-done(((f32[4,1,32768]{2,1,0:T(1,128)}), f32[4,1,32768]{2,1,0:T(1,128)S(1)}, u32[]{:S(2)}, u32[]{:S(2)}) %all-to-all-start.1) | async-done | bytes 524320 | tf_op jit(solution)/shard_map/all_to_all | solution.py:29
  42.6 2.1 %reduce.1 = f32[4,32768]{1,0:T(4,128)S(1)} reduce(f32[4,1,32768]{2,1,0:T(1,128)S(1)} %all-to-all-done.1, f32[]{:T(128)} %broadcast.76), dimensions={1}, to_apply=%all_to_all.30.reduce_sub_computation | reduce | bytes 1048580 | tf_op jit(solution)/shard_map/all_to_all | solution.py:29
  44.7 0.5 %reshape.40 = f32[128,16,64]{2,1,0:T(8,128)S(1)} reshape(f32[4,32768]{1,0:T(4,128)S(1)} %reduce.1) | data formatting | bytes 1048576
  45.2 0.7 %copy.17 = f32[16,32,4,64]{3,2,1,0:T(4,128)S(1)} copy(f32[16,32,4,64]{3,0,1,2:T(8,128)S(1)} %bitcast.26) | data formatting | bytes 1048576 | tf_op jit(solution)/shard_map/all_to_all | solution.py:29
  45.9 0.0 copy-start.1
  45.9 0.6 %all_to_all.33 = f32[16,32,256]{2,1,0:T(8,128)S(1)} reshape(f32[16,32,4,64]{3,2,1,0:T(4,128)S(1)} %copy.17) | data formatting | bytes 1048576 | tf_op jit(solution)/shard_map/all_to_all | solution.py:29
  46.6 0.1 copy-done.1
  46.6 2.4 %convolution_multiply_fusion = f32[16,32,256]{2,1,0:T(8,128)} fusion(f32[16,32,256]{2,1,0:T(8,128)S(1)} %all_to_all.33, f32[256]{0:T(256)S(1)} %copy-done.1, f32[16,32]{1,0:T(8,128)S(1)} %broadcast_add_fusion), kind=kOutput, calls=%fused_computation.1 | convolution fusion | flops 404488192 | bytes 1051648 | tf_op jit(solution)/shard_map/dot_general | solution.py:14
Async XLA Ops:
  0.0 1.0 %copy-start = (f32[128,16,64]{0,2,1:T(8,128)S(1)}, f32[128,16,64]{0,2,1:T(8,128)}, u32[]{:S(2)}) copy-start(f32[128,16,64]{0,2,1:T(8,128)} %param.4) | copy-start | bytes 1572868
  31.4 11.3 %all-to-all-start.1 = ((f32[4,1,32768]{2,1,0:T(1,128)}), f32[4,1,32768]{2,1,0:T(1,128)S(1)}, u32[]{:S(2)}, u32[]{:S(2)}) async-start(f32[4,1,32768]{2,1,0:T(1,128)} %reshape.39), calls=%async_computation.1 | async-start | bytes 1048576 | tf_op jit(solution)/shard_map/all_to_all | solution.py:29
  35.1 0.7 %copy-start.2 = (f32[128]{0:T(128)S(1)}, f32[128]{0:T(128)}, u32[]{:S(2)}) copy-start(f32[128]{0:T(128)} %param.6) | copy-start | bytes 1540
  35.8 0.7 %copy-start.3 = (f32[128]{0:T(128)S(1)}, f32[128]{0:T(128)}, u32[]{:S(2)}) copy-start(f32[128]{0:T(128)} %param.5) | copy-start | bytes 1540
  45.9 0.7 %copy-start.1 = (f32[256]{0:T(256)S(1)}, f32[256]{0:T(256)}, u32[]{:S(2)}) copy-start(f32[256]{0:T(256)} %param.7) | copy-start | bytes 3076
where the time goes:
time: 49.3 us; the launch traced here: 49 us
  blocking collectives  21.6 us (44%)
  local copies, waits for them, and re-layouts  8.49 us (17%)
  waiting for transfers between devices  6.04 us (12%)
  matrix products  5.17 us (10%)
  other arithmetic  3.92 us (8%)
  starting transfers between devices  3.72 us (8%)
    all_to_all x1, blocking collectives, first_leg(): lax.all_to_all(part_values, 'row', split_axis=0, concat_axis=1, tiled=True)  21.6 us
    all_to_all x1, waiting for transfers between devices, on_device(): lax.all_to_all(block_values, 'col', split_axis=1, concat_axis=2, tiled=True)  6.04 us
    unnamed x12, local copies, waits for them, and re-layouts  5.44 us
    dot_general x2, matrix products, transform_dim(): jnp.tensordot(values, mode_table(values.shape[dim]), axes=([dim], [0]), p...  4.33 us
    all_to_all x1, starting transfers between devices, on_device(): lax.all_to_all(block_values, 'col', split_axis=1, concat_axis=2, tiled=True)  3.72 us
    all_to_all x1, other arithmetic, on_device(): lax.all_to_all(block_values, 'col', split_axis=1, concat_axis=2, tiled=True)  2.05 us
    all_to_all x1, other arithmetic, first_leg(): lax.all_to_all(part_values, 'row', split_axis=0, concat_axis=1, tiled=True)  1.8 us
    all_to_all x2, local copies, waits for them, and re-layouts, on_device(): lax.all_to_all(block_values, 'col', split_axis=1, concat_axis=2, tiled=True)  1.29 us
  transfers between devices with their start and end apart: 1, of which 1 were waited for; matrix products, arithmetic and copies ran while one was open for 0% of the time, Pallas kernels for 0%

commit v1 on v0

v1 whole, which is shorter than its diff:
```python
import functools

import jax
import jax.numpy as jnp
import numpy as np
from jax import lax
from jax.experimental import pallas as pl
from jax.experimental.pallas import tpu as pltpu
from jax.sharding import PartitionSpec as P

MESH = pl.DeviceIdType.MESH
CHUNKS = 4


def mode_table(count):
    rank = np.arange(count, dtype=np.int64)
    angle = 2.0 * np.pi / count * (rank[:, None] * rank[None, :] % count)
    return ((np.cos(angle) + np.sin(angle)) * count ** (-0.5)).astype(np.float32)


def halves(table):
    high = table.astype(jnp.bfloat16)
    low = (table - high.astype(np.float32)).astype(jnp.bfloat16)
    return high, low


def split(values):
    high = values.astype(jnp.bfloat16)
    return high, (values - high.astype(jnp.float32)).astype(jnp.bfloat16)


def dot(a, b):
    return jnp.dot(a, b, preferred_element_type=jnp.float32)


def table_times(table_ref, values):
    rows = table_ref.shape[0] // 2
    high, low = split(values)
    both = dot(table_ref[...], high)
    return both[:rows] + both[rows:] + dot(table_ref[:rows], low)


def kernel(nr, nc, sx_ref, sy_ref, sz_ref, signal_ref, tx_ref, ty_ref, tzh_ref, tzl_ref, out_ref,
           sent, got, turned, lines, factor, spread, send_1, recv_1, send_2, recv_2):
    me_r, me_c = lax.axis_index("row"), lax.axis_index("col")
    dim_x, part_y, part_z = signal_ref.shape
    share_x, share_y, dim_z = out_ref.shape
    half = share_x // 2
    step = half // CHUNKS
    chips = nr // 2
    chip, core = me_r // 2, lax.rem(me_r, 2)
    far = chip >= chips // 2
    place = jnp.where(far, chips - 1 - chip, chip)

    def row_peer(index):
        if index == 0:
            return me_r + 1 - 2 * core
        ahead, other = 1 + (index - 1) // 2, (index - 1) % 2
        spot = lax.rem(place + ahead, chips)
        spot = jnp.where(far, chips - 1 - spot, spot)
        return spot * 2 + lax.rem(core + other, 2)

    row_peers = [row_peer(i) for i in range(nr - 1)]
    col_peers = [lax.rem(me_c + i, nc) for i in range(1, nc)]

    barrier = pltpu.get_barrier_semaphore()
    for peer in row_peers:
        pl.semaphore_signal(barrier, inc=1, device_id=(peer, me_c), device_id_type=MESH)
    for peer in col_peers:
        pl.semaphore_signal(barrier, inc=1, device_id=(me_r, peer), device_id_type=MESH)

    lane_half = part_y // 2
    pairs = dim_x // 2
    for q in range(0, lane_half, 2):
        many = min(2, lane_half - q)
        block = jnp.concatenate(
            [signal_ref[:, y, :] for i in range(many) for y in (q + i, q + i + lane_half)], axis=1)
        moved = table_times(tx_ref, block)
        for i in range(many):
            at = 2 * part_z * i
            first, second = moved[:pairs, at:at + 2 * part_z], moved[pairs:, at:at + 2 * part_z]
            sent[:, q + i, :] = jnp.concatenate([first[:, :part_z], second[:, :part_z]], axis=1)
            sent[:, q + i + lane_half, :] = jnp.concatenate([first[:, part_z:], second[:, part_z:]], axis=1)

    pl.semaphore_wait(barrier, nr - 1 + nc - 1)

    def row_copy(k, peer):
        return pltpu.make_async_remote_copy(
            src_ref=sent.at[pl.ds(peer * half + k * step, step)],
            dst_ref=got.at[pl.ds(k * step, step), pl.ds(me_r * part_y, part_y)],
            send_sem=send_1.at[k, peer], recv_sem=recv_1.at[k, me_r],
            device_id=(peer, me_c), device_id_type=MESH)

    def row_arrival(k, peer):
        return pltpu.make_async_remote_copy(
            src_ref=sent.at[pl.ds(peer * half + k * step, step)],
            dst_ref=got.at[pl.ds(k * step, step), pl.ds(peer * part_y, part_y)],
            send_sem=send_1.at[k, peer], recv_sem=recv_1.at[k, peer],
            device_id=(peer, me_c), device_id_type=MESH)

    def col_copy(k, peer):
        return pltpu.make_async_remote_copy(
            src_ref=turned.at[pl.ds(k * step, step), pl.ds(peer * share_y, share_y)],
            dst_ref=lines.at[me_c, pl.ds(k * step, step)],
            send_sem=send_2.at[k, peer], recv_sem=recv_2.at[k, me_c],
            device_id=(me_r, peer), device_id_type=MESH)

    def col_arrival(k, peer):
        return pltpu.make_async_remote_copy(
            src_ref=turned.at[pl.ds(k * step, step), pl.ds(peer * share_y, share_y)],
            dst_ref=lines.at[peer, pl.ds(k * step, step)],
            send_sem=send_2.at[k, peer], recv_sem=recv_2.at[k, peer],
            device_id=(me_r, peer), device_id_type=MESH)

    for k in range(CHUNKS):
        for peer in row_peers:
            row_copy(k, peer).start()

    got[:, pl.ds(pl.multiple_of(me_r * part_y, part_y), part_y), :] = sent[
        pl.ds(pl.multiple_of(me_r * half, half), half)]

    for i in range(share_y):
        spread[pl.ds(i, 1), :] = jnp.full((1, dim_z), sy_ref[me_c * share_y + i], jnp.float32)
    for i in range(share_x):
        symbol = (sx_ref[me_r * share_x + i] + spread[...]) + sz_ref[...]
        factor[i] = (1.0 - 0.2 * symbol) / (1.0 + 0.2 * symbol)

    def finish(k):
        for peer in col_peers:
            col_arrival(k, peer).wait_recv()
        parts = [lines[c, pl.ds(k * step, step)].reshape(step * share_y, 2 * part_z) for c in range(nc)]
        rows = jnp.concatenate(
            [jnp.concatenate([p[:, :part_z] for p in parts], axis=1),
             jnp.concatenate([p[:, part_z:] for p in parts], axis=1)], axis=0)
        high, low = split(rows)
        modes = dot(high, tzh_ref[...]) + (dot(low, tzh_ref[...]) + dot(high, tzl_ref[...]))
        modes = modes.reshape(2, step, share_y, dim_z)
        for side in range(2):
            at = pl.ds(side * half + k * step, step)
            out_ref[at] = modes[side] * factor[at]

    for k in range(CHUNKS):
        for peer in row_peers:
            row_arrival(k, peer).wait_recv()
        block = jnp.concatenate([got[k * step + j] for j in range(step)], axis=1)
        moved = table_times(ty_ref, block)
        for j in range(step):
            turned[k * step + j] = moved[:, 2 * part_z * j:2 * part_z * (j + 1)]
        for peer in col_peers:
            col_copy(k, peer).start()
        lines[me_c, pl.ds(k * step, step)] = turned[
            pl.ds(k * step, step), pl.ds(pl.multiple_of(me_c * share_y, share_y), share_y), :]
        if k > 0:
            finish(k - 1)
    finish(CHUNKS - 1)

    for k in range(CHUNKS):
        for peer in row_peers:
            row_copy(k, peer).wait_send()
        for peer in col_peers:
            col_copy(k, peer).wait_send()


def solution(mesh):
    nr, nc = mesh.shape["row"], mesh.shape["col"]

    def on_device(signal, symbol_x, symbol_y, symbol_z):
        dim_x, part_y, part_z = signal.shape
        dim_y, dim_z = part_y * nr, part_z * nc
        share_x, share_y = dim_x // nr, dim_y // nc
        half = share_x // 2
        order = np.arange(dim_x).reshape(nr, 2, half).transpose(1, 0, 2).reshape(-1)
        table_x = np.concatenate(halves(mode_table(dim_x)[order]), axis=0)
        table_y = np.concatenate(halves(mode_table(dim_y)), axis=0)
        table_zh, table_zl = halves(mode_table(dim_z))
        vmem, smem = pl.BlockSpec(memory_space=pltpu.VMEM), pl.BlockSpec(memory_space=pltpu.SMEM)
        wide = 2 * part_z
        return pl.pallas_call(
            functools.partial(kernel, nr, nc),
            out_shape=jax.ShapeDtypeStruct((share_x, share_y, dim_z), jnp.float32),
            in_specs=[smem, smem] + [vmem] * 6,
            out_specs=vmem,
            scratch_shapes=[
                pltpu.VMEM((nr * half, part_y, wide), jnp.float32),
                pltpu.VMEM((half, dim_y, wide), jnp.float32),
                pltpu.VMEM((half, dim_y, wide), jnp.float32),
                pltpu.VMEM((nc, half, share_y, wide), jnp.float32),
                pltpu.VMEM((share_x, share_y, dim_z), jnp.float32),
                pltpu.VMEM((share_y, dim_z), jnp.float32),
                pltpu.SemaphoreType.DMA((CHUNKS, nr)),
                pltpu.SemaphoreType.DMA((CHUNKS, nr)),
                pltpu.SemaphoreType.DMA((CHUNKS, nc)),
                pltpu.SemaphoreType.DMA((CHUNKS, nc)),
            ],
            compiler_params=pltpu.CompilerParams(
                collective_id=0, has_side_effects=True, vmem_limit_bytes=60 * 1024 * 1024),
        )(symbol_x, symbol_y, symbol_z.reshape(1, dim_z), signal,
          jnp.asarray(table_x), jnp.asarray(table_y), jnp.asarray(table_zh), jnp.asarray(table_zl))

    placed = (P(None, "row", "col"), P(), P(), P())
    return jax.shard_map(
        on_device, mesh=mesh, in_specs=placed, out_specs=P("row", "col", None), check_vma=False)
```

time: 49.3 us -> 32.7 us (0.66)
  Pallas kernels: 0 us -> 28.1 us
  blocking collectives: 21.6 us -> 0 us
  waiting for transfers between devices: 6.04 us -> 0 us
  matrix products: 5.17 us -> 0 us
  local copies, waits for them, and re-layouts: 8.49 us -> 4.31 us
  other arithmetic: 3.92 us -> 0 us
  starting transfers between devices: 3.72 us -> 0 us
    pallas_call x0 -> x1, Pallas kernels: none -> 28.1 us  [on_device(): pl.pallas_call(functools.partial(kernel, nr, nc), out_shape=jax.ShapeDtyp...]
    all_to_all x1 -> x0, blocking collectives: 21.6 us -> none  [first_leg(): lax.all_to_all(part_values, 'row', split_axis=0, concat_axis=1, tiled=True)]
    all_to_all x1 -> x0, waiting for transfers between devices: 6.04 us -> none  [on_device(): lax.all_to_all(block_values, 'col', split_axis=1, concat_axis=2, tiled=True)]
    dot_general x2 -> x0, matrix products: 4.33 us -> none  [transform_dim(): jnp.tensordot(values, mode_table(values.shape[dim]), axes=([dim], [0]), p...]
    all_to_all x2 -> x0, other arithmetic: 3.85 us -> none  [the longest x1 2.05 us: on_device(): lax.all_to_all(block_values, 'col', split_axis=1, concat_axis=2, tiled=True)]
    all_to_all x1 -> x0, starting transfers between devices: 3.72 us -> none  [on_device(): lax.all_to_all(block_values, 'col', split_axis=1, concat_axis=2, tiled=True)]
    all_to_all x4 -> x0, local copies, waits for them, and re-layouts: 1.91 us -> none  [the longest x2 1.29 us: on_device(): lax.all_to_all(block_values, 'col', split_axis=1, concat_axis=2, tiled=True)]
    unnamed x12 -> x2, local copies, waits for them, and re-layouts: 5.44 us -> 4.31 us
  transfers between devices with their start and end apart: 1 -> 0, of which waited for: 1 -> 0; matrix products, arithmetic and copies ran while one was open for 0% -> 0% of each run, Pallas kernels for 0% -> 0%
where the time goes in v1:
time: 32.7 us; the launch traced here: 32.4 us
  Pallas kernels  28.1 us (86%)
  local copies, waits for them, and re-layouts  4.31 us (13%)
    pallas_call x1, Pallas kernels, on_device(): pl.pallas_call(functools.partial(kernel, nr, nc), out_shape=jax.ShapeDtyp...  28.1 us
    unnamed x2, local copies, waits for them, and re-layouts  4.31 us

profile of v1, /device:TPU:0, one launch (start us, length us, event | category | flops | bytes accessed | tf_op | source)
XLA Modules:
  0.0 32.4 jit_solution(950274649090316389)
XLA Ops:
  0.0 2.4 %copy.9.signal_ref = f32[128,16,64]{2,1,0:T(8,128)} copy(f32[128,16,64]{0,2,1:T(8,128)} %param.8) | data formatting | bytes 1048576 | tf_op args[0]
  2.4 28.1 %shard_map.82 = f32[16,32,256]{2,1,0:T(8,128)} custom-call(f32[128]{0:T(128)} %sx_ref.1, f32[128]{0:T(128)} %sy_ref.1, f32[1,256]{1,0:T(1,128)} %bitcast.1, f32[128,16,64]{2,1,0:T(8,128)} %copy.9.signal_ref, bf16[256,128]{1,0:T(8,128)(2,1)} %constant.8.clone.tx_ref, bf16[256,128]{1,0:T(8,128)(2,1)} %constant.9.clone.ty_ref, ...), custom_call_target="tpu_custom_call" | custom-call | tf_op jit(solution)/shard_map/pallas_call | solution.py:178
  30.5 1.9 %copy.11 = f32[16,32,256]{2,1,0:T(8,128)} copy(f32[16,32,256]{2,1,0:T(8,128)} %shard_map.82) | data formatting | bytes 1048576

commit v2 on v1

--- a/solution.py
+++ b/solution.py
@@ -9,7 +9,9 @@
 from jax.sharding import PartitionSpec as P
 
 MESH = pl.DeviceIdType.MESH
-CHUNKS = 4
+SIZES = (5, 3,)
+CHUNKS = len(SIZES)
+LIMIT_SPARE = 8 * 1024 * 1024
 
 
 def mode_table(count):
@@ -33,20 +35,26 @@
     return jnp.dot(a, b, preferred_element_type=jnp.float32)
 
 
-def table_times(table_ref, values):
+def dot_rows(a, b):
+    return lax.dot_general(a, b, (((1,), (1,)), ((), ())), preferred_element_type=jnp.float32)
+
+
+def table_times(table_ref, values, product):
     rows = table_ref.shape[0] // 2
     high, low = split(values)
-    both = dot(table_ref[...], high)
-    return both[:rows] + both[rows:] + dot(table_ref[:rows], low)
-
-
-def kernel(nr, nc, sx_ref, sy_ref, sz_ref, signal_ref, tx_ref, ty_ref, tzh_ref, tzl_ref, out_ref,
-           sent, got, turned, lines, factor, spread, send_1, recv_1, send_2, recv_2):
+    both = product(table_ref[...], high)
+    return both[:rows] + both[rows:] + product(table_ref[:rows], low)
+
+
+def kernel(nr, nc, sx_ref, sy_ref, sz_ref, signal_far, tx_far, ty_far, tzh_far, tzl_far, out_far,
+           signal_ref, tx_ref, ty_ref, tzh_ref, tzl_ref, out_ref,
+           sent, got, turned, lines, factor, spread, send_1, recv_1, send_2, recv_2, in_sem, out_sem):
     me_r, me_c = lax.axis_index("row"), lax.axis_index("col")
-    dim_x, part_y, part_z = signal_ref.shape
+    part_y, part_z, dim_x = signal_ref.shape
     share_x, share_y, dim_z = out_ref.shape
     half = share_x // 2
-    step = half // CHUNKS
+    starts = [half * sum(SIZES[:k]) // sum(SIZES) for k in range(CHUNKS + 1)]
+    steps = [starts[k + 1] - starts[k] for k in range(CHUNKS)]
     chips = nr // 2
     chip, core = me_r // 2, lax.rem(me_r, 2)
     far = chip >= chips // 2
@@ -63,19 +71,28 @@
     row_peers = [row_peer(i) for i in range(nr - 1)]
     col_peers = [lax.rem(me_c + i, nc) for i in range(1, nc)]
 
+    loads = [
+        pltpu.make_async_copy(far_ref, near_ref, in_sem.at[i])
+        for i, (far_ref, near_ref) in enumerate(
+            ((signal_far, signal_ref), (tx_far, tx_ref), (ty_far, ty_ref), (tzh_far, tzh_ref), (tzl_far, tzl_ref)))]
+    for load in loads:
+        load.start()
+
     barrier = pltpu.get_barrier_semaphore()
     for peer in row_peers:
         pl.semaphore_signal(barrier, inc=1, device_id=(peer, me_c), device_id_type=MESH)
     for peer in col_peers:
         pl.semaphore_signal(barrier, inc=1, device_id=(me_r, peer), device_id_type=MESH)
 
+    loads[0].wait()
+    loads[1].wait()
     lane_half = part_y // 2
     pairs = dim_x // 2
     for q in range(0, lane_half, 2):
         many = min(2, lane_half - q)
         block = jnp.concatenate(
-            [signal_ref[:, y, :] for i in range(many) for y in (q + i, q + i + lane_half)], axis=1)
-        moved = table_times(tx_ref, block)
+            [signal_ref[y] for i in range(many) for y in (q + i, q + i + lane_half)], axis=0)
+        moved = table_times(tx_ref, block, dot_rows)
         for i in range(many):
             at = 2 * part_z * i
             first, second = moved[:pairs, at:at + 2 * part_z], moved[pairs:, at:at + 2 * part_z]
@@ -86,29 +103,29 @@
 
     def row_copy(k, peer):
         return pltpu.make_async_remote_copy(
-            src_ref=sent.at[pl.ds(peer * half + k * step, step)],
-            dst_ref=got.at[pl.ds(k * step, step), pl.ds(me_r * part_y, part_y)],
+            src_ref=sent.at[pl.ds(peer * half + starts[k], steps[k])],
+            dst_ref=got.at[pl.ds(starts[k], steps[k]), pl.ds(me_r * part_y, part_y)],
             send_sem=send_1.at[k, peer], recv_sem=recv_1.at[k, me_r],
             device_id=(peer, me_c), device_id_type=MESH)
 
     def row_arrival(k, peer):
         return pltpu.make_async_remote_copy(
-            src_ref=sent.at[pl.ds(peer * half + k * step, step)],
-            dst_ref=got.at[pl.ds(k * step, step), pl.ds(peer * part_y, part_y)],
+            src_ref=sent.at[pl.ds(peer * half + starts[k], steps[k])],
+            dst_ref=got.at[pl.ds(starts[k], steps[k]), pl.ds(peer * part_y, part_y)],
             send_sem=send_1.at[k, peer], recv_sem=recv_1.at[k, peer],
             device_id=(peer, me_c), device_id_type=MESH)
 
     def col_copy(k, peer):
         return pltpu.make_async_remote_copy(
-            src_ref=turned.at[pl.ds(k * step, step), pl.ds(peer * share_y, share_y)],
-            dst_ref=lines.at[me_c, pl.ds(k * step, step)],
+            src_ref=turned.at[pl.ds(starts[k], steps[k]), pl.ds(peer * share_y, share_y)],
+            dst_ref=lines.at[me_c, pl.ds(starts[k], steps[k])],
             send_sem=send_2.at[k, peer], recv_sem=recv_2.at[k, me_c],
             device_id=(me_r, peer), device_id_type=MESH)
 
     def col_arrival(k, peer):
         return pltpu.make_async_remote_copy(
-            src_ref=turned.at[pl.ds(k * step, step), pl.ds(peer * share_y, share_y)],
-            dst_ref=lines.at[peer, pl.ds(k * step, step)],
+            src_ref=turned.at[pl.ds(starts[k], steps[k]), pl.ds(peer * share_y, share_y)],
+            dst_ref=lines.at[peer, pl.ds(starts[k], steps[k])],
             send_sem=send_2.at[k, peer], recv_sem=recv_2.at[k, peer],
             device_id=(me_r, peer), device_id_type=MESH)
 
@@ -125,31 +142,41 @@
         symbol = (sx_ref[me_r * share_x + i] + spread[...]) + sz_ref[...]
         factor[i] = (1.0 - 0.2 * symbol) / (1.0 + 0.2 * symbol)
 
+    for load in loads[2:]:
+        load.wait()
+
+    def stores(k):
+        for side in range(2):
+            at = pl.ds(side * half + starts[k], steps[k])
+            yield pltpu.make_async_copy(out_ref.at[at], out_far.at[at], out_sem.at[k, side])
+
     def finish(k):
         for peer in col_peers:
             col_arrival(k, peer).wait_recv()
-        parts = [lines[c, pl.ds(k * step, step)].reshape(step * share_y, 2 * part_z) for c in range(nc)]
+        parts = [lines[c, pl.ds(starts[k], steps[k])].reshape(steps[k] * share_y, 2 * part_z) for c in range(nc)]
         rows = jnp.concatenate(
             [jnp.concatenate([p[:, :part_z] for p in parts], axis=1),
              jnp.concatenate([p[:, part_z:] for p in parts], axis=1)], axis=0)
         high, low = split(rows)
         modes = dot(high, tzh_ref[...]) + (dot(low, tzh_ref[...]) + dot(high, tzl_ref[...]))
-        modes = modes.reshape(2, step, share_y, dim_z)
+        modes = modes.reshape(2, steps[k], share_y, dim_z)
         for side in range(2):
-            at = pl.ds(side * half + k * step, step)
+            at = pl.ds(side * half + starts[k], steps[k])
             out_ref[at] = modes[side] * factor[at]
+        for store in stores(k):
+            store.start()
 
     for k in range(CHUNKS):
         for peer in row_peers:
             row_arrival(k, peer).wait_recv()
-        block = jnp.concatenate([got[k * step + j] for j in range(step)], axis=1)
-        moved = table_times(ty_ref, block)
-        for j in range(step):
-            turned[k * step + j] = moved[:, 2 * part_z * j:2 * part_z * (j + 1)]
+        block = jnp.concatenate([got[starts[k] + j] for j in range(steps[k])], axis=1)
+        moved = table_times(ty_ref, block, dot)
+        for j in range(steps[k]):
+            turned[starts[k] + j] = moved[:, 2 * part_z * j:2 * part_z * (j + 1)]
         for peer in col_peers:
             col_copy(k, peer).start()
-        lines[me_c, pl.ds(k * step, step)] = turned[
-            pl.ds(k * step, step), pl.ds(pl.multiple_of(me_c * share_y, share_y), share_y), :]
+        lines[me_c, pl.ds(starts[k], steps[k])] = turned[
+            pl.ds(starts[k], steps[k]), pl.ds(pl.multiple_of(me_c * share_y, share_y), share_y), :]
         if k > 0:
             finish(k - 1)
     finish(CHUNKS - 1)
@@ -159,6 +186,8 @@
             row_copy(k, peer).wait_send()
         for peer in col_peers:
             col_copy(k, peer).wait_send()
+        for store in stores(k):
+            store.wait()
 
 
 def solution(mesh):
@@ -174,13 +203,21 @@
         table_y = np.concatenate(halves(mode_table(dim_y)), axis=0)
         table_zh, table_zl = halves(mode_table(dim_z))
         vmem, smem = pl.BlockSpec(memory_space=pltpu.VMEM), pl.BlockSpec(memory_space=pltpu.SMEM)
+        far = pl.BlockSpec(memory_space=pltpu.HBM)
+        result = pl.BlockSpec(memory_space=pl.ANY)
         wide = 2 * part_z
+        tables = [jnp.asarray(t) for t in (table_x, table_y, table_zh, table_zl)]
+        out_shape = (share_x, share_y, dim_z)
+        limit = 7 * signal.size * 4 + sum(t.size * 2 for t in tables) + LIMIT_SPARE
         return pl.pallas_call(
             functools.partial(kernel, nr, nc),
-            out_shape=jax.ShapeDtypeStruct((share_x, share_y, dim_z), jnp.float32),
-            in_specs=[smem, smem] + [vmem] * 6,
-            out_specs=vmem,
+            out_shape=jax.ShapeDtypeStruct(out_shape, jnp.float32),
+            in_specs=[smem, smem, vmem] + [far] * 5,
+            out_specs=result,
             scratch_shapes=[
+                pltpu.VMEM((part_y, part_z, dim_x), jnp.float32),
+                *[pltpu.VMEM(t.shape, t.dtype) for t in tables],
+                pltpu.VMEM(out_shape, jnp.float32),
                 pltpu.VMEM((nr * half, part_y, wide), jnp.float32),
                 pltpu.VMEM((half, dim_y, wide), jnp.float32),
                 pltpu.VMEM((half, dim_y, wide), jnp.float32),
@@ -191,11 +228,12 @@
                 pltpu.SemaphoreType.DMA((CHUNKS, nr)),
                 pltpu.SemaphoreType.DMA((CHUNKS, nc)),
                 pltpu.SemaphoreType.DMA((CHUNKS, nc)),
+                pltpu.SemaphoreType.DMA((5,)),
+                pltpu.SemaphoreType.DMA((CHUNKS, 2)),
             ],
             compiler_params=pltpu.CompilerParams(
                 collective_id=0, has_side_effects=True, vmem_limit_bytes=60 * 1024 * 1024),
-        )(symbol_x, symbol_y, symbol_z.reshape(1, dim_z), signal,
-          jnp.asarray(table_x), jnp.asarray(table_y), jnp.asarray(table_zh), jnp.asarray(table_zl))
+        )(symbol_x, symbol_y, symbol_z.reshape(1, dim_z), signal.transpose(1, 2, 0), *tables)
 
     placed = (P(None, "row", "col"), P(), P(), P())
     return jax.shard_map(

time: 32.7 us -> 27.6 us (0.84)
  Pallas kernels: 28.1 us -> 25.5 us
  local copies, waits for them, and re-layouts: 4.31 us -> 1.88 us
    pallas_call x1, Pallas kernels: 28.1 us -> 25.5 us  [on_device(): pl.pallas_call(functools.partial(kernel, nr, nc), out_shape=jax.ShapeDtyp...]
    unnamed x2 -> x1, local copies, waits for them, and re-layouts: 4.31 us -> 1.88 us
where the time goes in v2:
time: 27.6 us; the launch traced here: 27.4 us
  Pallas kernels  25.5 us (92%)
  local copies, waits for them, and re-layouts  1.88 us (7%)
    pallas_call x1, Pallas kernels, on_device(): pl.pallas_call(functools.partial(kernel, nr, nc), out_shape=jax.ShapeDtyp...  25.5 us
    unnamed x1, local copies, waits for them, and re-layouts  1.88 us

profile of v2, /device:TPU:0, one launch (start us, length us, event | category | flops | bytes accessed | tf_op | source)
XLA Modules:
  0.0 27.4 jit_solution(4474563482885326269)
XLA Ops:
  0.0 25.5 %shard_map.82 = f32[16,32,256]{2,1,0:T(8,128)} custom-call(f32[128]{0:T(128)} %sx_ref.1, f32[128]{0:T(128)} %sy_ref.1, f32[1,256]{1,0:T(1,128)} %bitcast.3, f32[16,64,128]{2,1,0:T(8,128)} %bitcast.2, bf16[256,128]{1,0:T(8,128)(2,1)} %constant.8.clone.tx_far, bf16[256,128]{1,0:T(8,128)(2,1)} %constant.9.clone.ty_far, ...), custom_call_target="tpu_custom_call" | custom-call | tf_op jit(solution)/shard_map/pallas_call | solution.py:212
  25.5 1.9 %copy.10 = f32[16,32,256]{2,1,0:T(8,128)} copy(f32[16,32,256]{2,1,0:T(8,128)} %shard_map.82) | data formatting | bytes 1048576
